TPU v7x, 256 devices: a whole 4x4x8 slice. The times are simulated.
256 devices in a mesh: dp: 8 (over z_hi, x), ha: 4 (over y), wa: 8 (over z_lo, core).
Axes of the slice: x: 4, y: 4, z: 8 (z_hi: 2, z_lo: 4; z = z_hi * 4 + z_lo), core: 2. Of those that a mesh axis runs over, the one named last changes fastest.
Arguments:
- queries: bfloat16 [8, 1, 4, 8, 144, 768], P('dp', None, 'ha', 'wa'), may hold values from -5 to 5
- key_tiles: bfloat16 [8, 1, 4, 8, 144, 768], P('dp', None, 'ha', 'wa'), may hold values from -5 to 5
- value_tiles: bfloat16 [8, 1, 4, 8, 144, 768], P('dp', None, 'ha', 'wa'), may hold values from -6 to 6
- out_grad: bfloat16 [8, 1, 4, 8, 144, 1536], P('dp', None, 'ha', 'wa'), may hold values from -8 to 8
- w_out: bfloat16 [1536, 768], replicated, may hold values from -0.21875 to 0.21875
- reaches: int32 [6, 6], replicated, may hold values from 0 to 1, as said below
Outputs:
- grad_query: bfloat16 [8, 1, 4, 8, 144, 768], P('dp', None, 'ha', 'wa')
- grad_key: bfloat16 [8, 1, 4, 8, 144, 768], P('dp', None, 'ha', 'wa')
- grad_value: bfloat16 [8, 1, 4, 8, 144, 768], P('dp', None, 'ha', 'wa')
- grad_w_out: float32 [1536, 768], P(('dp', 'ha', 'wa'))
Inputs may be any that keep to these rules, and one draw needn't show every extreme that they name: `reaches`: some head has every entry 1, and some other head has every entry 0.
All inputs are finite; a program needn't handle non-finite values.
Results may differ from a plain program's by a relative error of at most 0.018.
Values may be sent and summed in bfloat16 or wider, within the bound.
No kernel may reach another device: no remote copies, remote signals or barrier semaphores. Data moves between devices by JAX's collectives and lax.ppermute only.
A program may use at most 128 MiB of HBM per device.

v0:
```python
import math

import jax
import jax.numpy as jnp
from jax import lax
from jax.sharding import PartitionSpec as P

HEADS = 6
HD = 128


def shifted(block, axis, distance):
    devices = range(lax.axis_size(axis))
    route = [(i - distance, i) for i in devices if i - distance in devices]
    return lax.ppermute(block, axis, route)


def padded_2(array, sides, width):
    for axis, dim in sides:
        size, length = (lax.axis_size(axis), array.shape[dim])
        up = [(i, (i + 1) % size) for i in range(size - 1)]
        down = [(j, i) for i, j in up]
        last = lax.slice_in_dim(array, length - width, length, axis=dim)
        initial = lax.slice_in_dim(array, 0, width, axis=dim)
        before = lax.ppermute(last, axis, up)
        after = lax.ppermute(initial, axis, down)
        array = jnp.concatenate([before, array, after], axis=dim)
    return array


def split_up(array, dim, size):
    shape = array.shape
    parts = array.reshape(*shape[:dim], size, shape[dim] // size, *shape[dim + 1 :])
    return jnp.moveaxis(parts, dim, 0)


def sent_and_summed(array, axis, dim):
    size = lax.axis_size(axis)
    parts = lax.all_to_all(split_up(array, dim, size), axis, 0, 0, tiled=True)
    return jnp.sum(parts.astype(jnp.float32), axis=0)


def sum_at_owner(array, axis, dim):
    size = lax.axis_size(axis)
    parts = lax.all_to_all(split_up(array, dim, size), axis, 0, 0, tiled=True)
    return jnp.sum(parts, axis=0)


def tile_allowed(reach_row, t_count, row_base, col_base, row_total, col_total):
    time_ids = jnp.arange(t_count)
    t_delta = time_ids[None, :] - time_ids[:, None]
    time_ok = (t_delta >= -reach_row[0]) & (t_delta <= reach_row[1])
    offsets = jnp.arange(3) - 1
    row_ok = (
        (offsets >= -reach_row[2])
        & (offsets <= reach_row[3])
        & (row_base + offsets >= 0)
        & (row_base + offsets < row_total)
    )
    col_ok = (
        (offsets >= -reach_row[4])
        & (offsets <= reach_row[5])
        & (col_base + offsets >= 0)
        & (col_base + offsets < col_total)
    )
    return time_ok[:, :, None, None] & row_ok[None, None, :, None] & col_ok[None, None, None, :]


def pass_along_width(edge_piece, offset):
    return shifted(edge_piece.astype(jnp.bfloat16), "wa", offset).astype(edge_piece.dtype)


def pass_along_height(edge_piece, offset):
    return shifted(edge_piece.astype(jnp.bfloat16), "ha", offset).astype(edge_piece.dtype)


def shards(queries, key_tiles, value_tiles, out_grad, w_out, reaches):
    t_count = queries.shape[1]
    tile_len = queries.shape[4]
    width_q = queries.shape[5]
    model_width = out_grad.shape[5]
    token_rows = t_count * tile_len
    key_count = t_count * 9 * tile_len
    softmax_scale = 1.0 / math.sqrt(HD)
    row_base = lax.axis_index("ha")
    col_base = lax.axis_index("wa")
    row_total = lax.axis_size("ha")
    col_total = lax.axis_size("wa")
    key_value = jnp.concatenate([key_tiles, value_tiles], axis=5)
    padded = padded_2(key_value, (("ha", 2), ("wa", 3)), 1)
    padded = padded.reshape(key_count, 2 * width_q)
    query_rows = queries.reshape(token_rows, width_q)
    grad_rows = out_grad.reshape(token_rows, model_width)
    grad_attn = jnp.dot(grad_rows, w_out, preferred_element_type=jnp.float32).astype(jnp.bfloat16)
    attn_list, gq_list, gk_list, gv_list = ([], [], [], [])
    for head_index in range(HEADS):
        col_start = head_index * HD
        col_stop = col_start + HD
        query_head = query_rows[:, col_start:col_stop]
        key_head = padded[:, col_start:col_stop]
        value_head = padded[:, width_q + col_start : width_q + col_stop]
        grad_head = grad_attn[:, col_start:col_stop]
        tile_pairs = tile_allowed(
            reaches[head_index], t_count, row_base, col_base, row_total, col_total
        )
        allowed = jnp.broadcast_to(
            tile_pairs[:, None, :, :, :, None], (t_count, tile_len, t_count, 3, 3, tile_len)
        ).reshape(token_rows, key_count)
        scores = (
            jnp.einsum("ad,bd->ab", query_head, key_head, preferred_element_type=jnp.float32)
            * softmax_scale
        )
        masked = jnp.where(allowed, scores, -jnp.inf)
        row_peak = jnp.max(masked, axis=1, keepdims=True)
        exp_terms = jnp.exp(masked - row_peak)
        prob_rows = exp_terms / jnp.sum(exp_terms, axis=1, keepdims=True)
        probs_low = prob_rows.astype(jnp.bfloat16)
        attn_head = jnp.dot(probs_low, value_head, preferred_element_type=jnp.float32).astype(
            jnp.bfloat16
        )
        row_delta = jnp.sum(
            grad_head.astype(jnp.float32) * attn_head.astype(jnp.float32), axis=1, keepdims=True
        )
        grad_probs = jnp.einsum(
            "ad,bd->ab", grad_head, value_head, preferred_element_type=jnp.float32
        )
        grad_scores = (prob_rows * (grad_probs - row_delta)).astype(jnp.bfloat16)
        grad_q_head = (
            jnp.dot(grad_scores, key_head, preferred_element_type=jnp.float32) * softmax_scale
        ).astype(jnp.bfloat16)
        grad_k_head = (
            jnp.einsum("ab,ad->bd", grad_scores, query_head, preferred_element_type=jnp.float32)
            * softmax_scale
        )
        grad_v_head = jnp.einsum(
            "ab,ad->bd", probs_low, grad_head, preferred_element_type=jnp.float32
        )
        attn_list.append(attn_head)
        gq_list.append(grad_q_head)
        gk_list.append(grad_k_head)
        gv_list.append(grad_v_head)
    attended = jnp.concatenate(attn_list, axis=1)
    grad_query = jnp.concatenate(gq_list, axis=1).reshape(queries.shape)
    partial_value = jnp.concatenate(gk_list + gv_list, axis=1).reshape(
        t_count, 3, 3, tile_len, 2 * width_q
    )
    from_right = pass_along_width(partial_value[:, :, 0], -1)
    from_left = pass_along_width(partial_value[:, :, 2], 1)
    middle = partial_value[:, :, 1] + from_right + from_left
    summed = middle[:, 1] + pass_along_height(middle[:, 0], -1) + pass_along_height(middle[:, 2], 1)
    grad_key = summed[:, :, :width_q].astype(jnp.bfloat16).reshape(queries.shape)
    grad_value = summed[:, :, width_q:].astype(jnp.bfloat16).reshape(queries.shape)
    coarse = sent_and_summed(
        lax.dot_general(
            grad_rows, attended, (((0,), (0,)), ((), ())), preferred_element_type=jnp.float32
        ).astype(jnp.bfloat16),
        "dp",
        0,
    )
    grad_w_out = sum_at_owner(coarse, ("ha", "wa"), 0)
    return (grad_query, grad_key, grad_value, grad_w_out)


def solution(mesh):
    in_specs = (
        P("dp", None, "ha", "wa", None, None),
        P("dp", None, "ha", "wa", None, None),
        P("dp", None, "ha", "wa", None, None),
        P("dp", None, "ha", "wa", None, None),
        P(),
        P(),
    )
    out_specs = (
        P("dp", None, "ha", "wa", None, None),
        P("dp", None, "ha", "wa", None, None),
        P("dp", None, "ha", "wa", None, None),
        P(("dp", "ha", "wa"), None),
    )
    return jax.shard_map(shards, mesh=mesh, in_specs=in_specs, out_specs=out_specs, check_vma=False)
```

profile of v0, /device:TPU:1, one launch (start us, length us, event | category | flops | bytes accessed | tf_op | source)
XLA Modules:
  0.0 191.5 jit_solution(6622777393933172297)
XLA Ops:
  4.0 5.4 %collective-permute-start = (bf16[1,1,1,1,144,1536]{5,4,3,2,1,0:T(8,128)(2,1)S(1)}, bf16[1,1,1,1,144,1536]{5,4,3,2,1,0:T(8,128)(2,1)}, u32[]{:S(2)}, u32[]{:S(2)}) collective-permute-start(bf16[1,1,1,1,144,1536]{5,4,3,2,1,0:T(8,128)(2,1)S(1)} %constant_dynamic-update-slice_fusion), channel_id=1, source_target_pairs={{0,8},{8,16},{16,24},{1,9},{9,17},{17,25},{2,10},{10,18},{18,26},{... | collective-permute-start | bytes 1327112 | tf_op jit(solution)/shard_map/ppermute | solution.py:25
  9.4 2.0 %fusion.125 = (s32[1,1]{1,0:T(1,128)}, s32[1,1]{1,0:T(1,128)}, s32[1,1]{1,0:T(1,128)}, s32[1,1]{1,0:T(1,128)}, s32[1,1]{1,0:T(1,128)}, /*index=5*/s32[1,1]{1,0:T...) fusion(s32[6,6]{1,0:T(8,128)} %param.11), kind=kLoop, calls=%fused_computation.207 | loop fusion | bytes 136 | tf_op jit(solution)/shard_map/slice | solution.py:55
  22.1 2.1 %fusion.124 = (s32[1,1]{1,0:T(1,128)}, s32[1,1]{1,0:T(1,128)}, s32[1,1]{1,0:T(1,128)}, s32[1,1]{1,0:T(1,128)}, s32[1,1]{1,0:T(1,128)}, /*index=5*/s32[1,1]{1,0:T...) fusion(s32[6,6]{1,0:T(8,128)} %param.11), kind=kLoop, calls=%fused_computation.206 | loop fusion | bytes 152 | tf_op jit(solution)/shard_map/slice | solution.py:55
  34.5 2.4 %pad_maximum_fusion.1 = bf16[1,1,3,1,144,1536]{5,4,3,2,1,0:T(8,128)(2,1)} fusion(bf16[1,1,1,1,144,1536]{5,4,3,2,1,0:T(8,128)(2,1)} %collective-permute-done.1, bf16[1,1,1,1,144,1536]{5,4,3,2,1,0:T(8,128)(2,1)S(1)} %constant_dynamic-update-slice_fusion, bf16[1,1,1,1,144,1536]{5,4,3,2,1,0:T(8,128)(2,1)} %collective-permute-done), kind=kLoop, calls=%fused_computation.57 | loop fusion | flops 1327104 | bytes 2654208 | tf_op jit(solution)/shard_map/concatenate | solution.py:27
  36.8 5.0 %collective-permute-start.3 = (bf16[1,1,3,1,144,1536]{5,4,3,2,1,0:T(8,128)(2,1)}, bf16[1,1,3,1,144,1536]{5,4,3,2,1,0:T(8,128)(2,1)}, u32[]{:S(2)}, u32[]{:S(2)}) collective-permute-start(bf16[1,1,3,1,144,1536]{5,4,3,2,1,0:T(8,128)(2,1)} %pad_maximum_fusion.1), channel_id=1, source_target_pairs={{1,0},{2,1},{3,2},{4,3},{5,4},{6,5},{7,6},{9,8},{10,9},{11,10},{12... | collective-permute-start | bytes 3981320 | tf_op jit(solution)/shard_map/ppermute | solution.py:26
  41.9 1.9 %collective-permute-start.2 = (bf16[1,1,3,1,144,1536]{5,4,3,2,1,0:T(8,128)(2,1)}, bf16[1,1,3,1,144,1536]{5,4,3,2,1,0:T(8,128)(2,1)}, u32[]{:S(2)}, u32[]{:S(2)}) collective-permute-start(bf16[1,1,3,1,144,1536]{5,4,3,2,1,0:T(8,128)(2,1)} %pad_maximum_fusion.1), channel_id=1, source_target_pairs={{0,1},{1,2},{2,3},{3,4},{4,5},{5,6},{6,7},{8,9},{9,10},{10,11},{11... | collective-permute-start | bytes 3981320 | tf_op jit(solution)/shard_map/ppermute | solution.py:25
  47.9 9.6 %collective-permute-done.3 = bf16[1,1,3,1,144,1536]{5,4,3,2,1,0:T(8,128)(2,1)} collective-permute-done((bf16[1,1,3,1,144,1536]{5,4,3,2,1,0:T(8,128)(2,1)}, bf16[1,1,3,1,144,1536]{5,4,3,2,1,0:T(8,128)(2,1)}, u32[]{:S(2)}, u32[]{:S(2)}) %collective-permute-start.3) | collective-permute-done | bytes 1327136 | tf_op jit(solution)/shard_map/ppermute | solution.py:26
  58.8 2.2 %pad_maximum_fusion = bf16[1,1,3,3,144,1536]{5,4,3,2,1,0:T(8,128)(2,1)S(1)} fusion(bf16[1,1,3,1,144,1536]{5,4,3,2,1,0:T(8,128)(2,1)} %collective-permute-done.3, bf16[1,1,1,1,144,1536]{5,4,3,2,1,0:T(8,128)(2,1)} %collective-permute-done.1, bf16[1,1,1,1,144,1536]{5,4,3,2,1,0:T(8,128)(2,1)S(1)} %constant_dynamic-update-slice_fusion, ...), kind=kLoop, calls=%fused_computation.1 | loop fusion | flops 7962624 | bytes 7962624 | tf_op jit(solution)/shard_map/concatenate | solution.py:27
  73.1 2.3 %fusion = bf16[1536,768]{0,1:T(8,128)(2,1)} fusion(bf16[144,768]{1,0:T(8,128)(2,1)S(1)} %constant_dynamic-update-slice_fusion.2, bf16[1,1,1,1,144,1536]{5,4,3,2,1,0:T(8,128)(2,1)S(1)} %copy-done.2), kind=kOutput, calls=%fused_computation.3 | convolution fusion | flops 340918272 | bytes 3022848 | tf_op jit(solution)/shard_map/dot_general | solution.py:154
  75.4 4.4 %copy.14 = bf16[1536,768]{1,0:T(8,128)(2,1)} copy(bf16[1536,768]{0,1:T(8,128)(2,1)} %fusion) | data formatting | bytes 4718592 | tf_op jit(solution)/shard_map/convert_element_type | solution.py:156
  79.7 9.7 %all-to-all-start = ((bf16[8,192,768]{2,1,0:T(8,128)(2,1)}), bf16[8,192,768]{2,1,0:T(8,128)(2,1)}, u32[]{:S(2)}, u32[]{:S(2)}) async-start(bf16[8,192,768]{2,1,0:T(8,128)(2,1)} %bitcast.125), calls=%async_computation | async-start | bytes 4718592 | tf_op jit(solution)/shard_map/all_to_all | solution.py:39
  89.5 1.5 fusion.20
  92.3 1.5 fusion.18
  99.8 1.9 %collective-permute-start.4 = (bf16[1,3,144,1536]{3,2,1,0:T(8,128)(2,1)S(1)}, bf16[1,3,144,1536]{3,2,1,0:T(8,128)(2,1)S(1)}, u32[]{:S(2)}, u32[]{:S(2)}) collective-permute-start(bf16[1,3,144,1536]{3,2,1,0:T(8,128)(2,1)S(1)} %get-tuple-element.12), channel_id=1, source_target_pairs={{1,0},{2,1},{3,2},{4,3},{5,4},{6,5},{7,6},{9,8},{10,9},{11,10},{12... | collective-permute-start | bytes 3981320 | tf_op jit(solution)/shard_map/ppermute | solution.py:15
  101.7 4.7 %collective-permute-start.5 = (bf16[1,3,144,1536]{3,2,1,0:T(8,128)(2,1)S(1)}, bf16[1,3,144,1536]{3,2,1,0:T(8,128)(2,1)S(1)}, u32[]{:S(2)}, u32[]{:S(2)}) collective-permute-start(bf16[1,3,144,1536]{3,2,1,0:T(8,128)(2,1)S(1)} %get-tuple-element.13), channel_id=1, source_target_pairs={{0,1},{1,2},{2,3},{3,4},{4,5},{5,6},{6,7},{8,9},{9,10},{10,11},{11... | collective-permute-start | bytes 3981320 | tf_op jit(solution)/shard_map/ppermute | solution.py:15
  111.5 35.0 %collective-permute-done.4 = bf16[1,3,144,1536]{3,2,1,0:T(8,128)(2,1)S(1)} collective-permute-done((bf16[1,3,144,1536]{3,2,1,0:T(8,128)(2,1)S(1)}, bf16[1,3,144,1536]{3,2,1,0:T(8,128)(2,1)S(1)}, u32[]{:S(2)}, u32[]{:S(2)}) %collective-permute-start.4) | collective-permute-done | bytes 1327136 | tf_op jit(solution)/shard_map/ppermute | solution.py:15
  146.5 2.2 %fusion.122 = (bf16[1,3,144,1536]{3,2,1,0:T(8,128)(2,1)S(1)}, f32[1,3,144,1536]{3,2,1,0:T(8,128)}) fusion(bf16[1,3,144,1536]{3,2,1,0:T(8,128)(2,1)S(1)} %collective-permute-done.5, bf16[1,3,144,1536]{3,2,1,0:T(8,128)(2,1)S(1)} %collective-permute-done.4, f32[1,3,3,144,1536]{4,3,2,1,0:T(8,128)S(1)} %bitcast.127), kind=kLoop, calls=%fused_computation.205 | loop fusion | flops 3317760 | bytes 9289728 | tf_op jit(solution)/shard_map/convert.3
  150.9 4.8 %collective-permute-start.7 = (bf16[1,144,1536]{2,1,0:T(8,128)(2,1)}, bf16[1,144,1536]{2,1,0:T(8,128)(2,1)}, u32[]{:S(2)}, u32[]{:S(2)}) collective-permute-start(bf16[1,144,1536]{2,1,0:T(8,128)(2,1)} %get-tuple-element.15), channel_id=1, source_target_pairs={{0,8},{8,16},{16,24},{1,9},{9,17},{17,25},{2,10},{10,18},{18,26},{... | collective-permute-start | bytes 1327112 | tf_op jit(solution)/shard_map/ppermute | solution.py:15
  155.7 2.0 %convert_reduce_fusion = f32[192,768]{1,0:T(8,128)S(1)} fusion(bf16[8,192,768]{2,1,0:T(8,128)(2,1)} %all-to-all-done), kind=kLoop, calls=%fused_computation | loop fusion | flops 2211840 | bytes 2949120 | tf_op jit(solution)/shard_map/reduce_sum | solution.py:40
  158.8 9.7 %all-to-all-start.1 = ((f32[32,6,768]{2,1,0:T(8,128)}), f32[32,6,768]{2,1,0:T(8,128)S(1)}, u32[]{:S(2)}, u32[]{:S(2)}) async-start(f32[32,6,768]{2,1,0:T(8,128)} %reshape.621), calls=%async_computation.1 | async-start | bytes 1572864 | tf_op jit(solution)/shard_map/all_to_all | solution.py:45
  168.5 2.0 %fusion.36 = bf16[144,768]{1,0:T(8,128)(2,1)} fusion(bf16[144,768]{1,0:T(8,128)(2,1)} %copy-done.25, bf16[144,1296]{1,0:T(8,128)(2,1)} %fusion.25, bf16[1296,1536]{1,0:T(8,128)(2,1)} %bitcast.150), kind=kOutput, calls=%fused_computation.74 | convolution fusion | flops 47812608 | bytes 774144 | tf_op jit(solution)/shard_map/dot_general | solution.py:129
  170.5 1.9 fusion.38
  172.4 1.6 fusion.41
  174.7 16.1 %all-to-all-done.1 = f32[32,6,768]{2,1,0:T(8,128)S(1)} async-done(((f32[32,6,768]{2,1,0:T(8,128)}), f32[32,6,768]{2,1,0:T(8,128)S(1)}, u32[]{:S(2)}, u32[]{:S(2)}) %all-to-all-start.1) | async-done | bytes 589856 | tf_op jit(solution)/shard_map/all_to_all | solution.py:45
  (132 shorter events, 43.3 us)
Async XLA Ops:
  0.6 46.7 %copy-start = (bf16[1536,768]{1,0:T(8,128)(2,1)S(1)}, bf16[1536,768]{1,0:T(8,128)(2,1)}, u32[]{:S(2)}) copy-start(bf16[1536,768]{1,0:T(8,128)(2,1)} %param.10) | copy-start | bytes 7077892
  0.6 46.7 %copy-start.2 = (bf16[1,1,1,1,144,1536]{5,4,3,2,1,0:T(8,128)(2,1)S(1)}, bf16[1,1,1,1,144,1536]{5,4,3,2,1,0:T(8,128)(2,1)}, u32[]{:S(2)}) copy-start(bf16[1,1,1,1,144,1536]{5,4,3,2,1,0:T(8,128)(2,1)} %param.9) | copy-start | bytes 1327108
  2.7 31.7 %collective-permute-start.1 = (bf16[1,1,1,1,144,1536]{5,4,3,2,1,0:T(8,128)(2,1)S(1)}, bf16[1,1,1,1,144,1536]{5,4,3,2,1,0:T(8,128)(2,1)}, u32[]{:S(2)}, u32[]{:S(2)}) collective-permute-start(bf16[1,1,1,1,144,1536]{5,4,3,2,1,0:T(8,128)(2,1)S(1)} %constant_dynamic-update-slice_fusion), channel_id=1, source_target_pairs={{8,0},{16,8},{24,16},{9,1},{17,9},{25,17},{10,2},{18,10},{26,18},{... | collective-permute-start | bytes 1327112 | tf_op jit(solution)/shard_map/ppermute | solution.py:26
  4.0 30.4 %collective-permute-start = (bf16[1,1,1,1,144,1536]{5,4,3,2,1,0:T(8,128)(2,1)S(1)}, bf16[1,1,1,1,144,1536]{5,4,3,2,1,0:T(8,128)(2,1)}, u32[]{:S(2)}, u32[]{:S(2)}) collective-permute-start(bf16[1,1,1,1,144,1536]{5,4,3,2,1,0:T(8,128)(2,1)S(1)} %constant_dynamic-update-slice_fusion), channel_id=1, source_target_pairs={{0,8},{8,16},{16,24},{1,9},{9,17},{17,25},{2,10},{10,18},{18,26},{... | collective-permute-start | bytes 1327112 | tf_op jit(solution)/shard_map/ppermute | solution.py:25
  36.8 20.6 %collective-permute-start.3 = (bf16[1,1,3,1,144,1536]{5,4,3,2,1,0:T(8,128)(2,1)}, bf16[1,1,3,1,144,1536]{5,4,3,2,1,0:T(8,128)(2,1)}, u32[]{:S(2)}, u32[]{:S(2)}) collective-permute-start(bf16[1,1,3,1,144,1536]{5,4,3,2,1,0:T(8,128)(2,1)} %pad_maximum_fusion.1), channel_id=1, source_target_pairs={{1,0},{2,1},{3,2},{4,3},{5,4},{6,5},{7,6},{9,8},{10,9},{11,10},{12... | collective-permute-start | bytes 3981320 | tf_op jit(solution)/shard_map/ppermute | solution.py:26
  41.9 17.0 %collective-permute-start.2 = (bf16[1,1,3,1,144,1536]{5,4,3,2,1,0:T(8,128)(2,1)}, bf16[1,1,3,1,144,1536]{5,4,3,2,1,0:T(8,128)(2,1)}, u32[]{:S(2)}, u32[]{:S(2)}) collective-permute-start(bf16[1,1,3,1,144,1536]{5,4,3,2,1,0:T(8,128)(2,1)} %pad_maximum_fusion.1), channel_id=1, source_target_pairs={{0,1},{1,2},{2,3},{3,4},{4,5},{5,6},{6,7},{8,9},{9,10},{10,11},{11... | collective-permute-start | bytes 3981320 | tf_op jit(solution)/shard_map/ppermute | solution.py:25
  47.8 24.1 %copy-start.23 = (bf16[144,768]{1,0:T(8,128)(2,1)}, bf16[144,768]{1,0:T(8,128)(2,1)S(1)}, u32[]{:S(2)}) copy-start(bf16[144,768]{1,0:T(8,128)(2,1)S(1)} %convolution_convert_fusion.1) | copy-start | bytes 663556
  47.9 13.2 %copy-start.22 = (bf16[1,1,1,1,144,768]{5,4,3,2,1,0:T(8,128)(2,1)S(1)}, bf16[1,1,1,1,144,768]{5,4,3,2,1,0:T(8,128)(2,1)}, u32[]{:S(2)}) copy-start(bf16[1,1,1,1,144,768]{5,4,3,2,1,0:T(8,128)(2,1)} %param.6) | copy-start | bytes 663556
  61.0 11.0 %copy-start.1 = (bf16[1,1,3,3,144,1536]{5,4,3,2,1,0:T(8,128)(2,1)}, bf16[1,1,3,3,144,1536]{5,4,3,2,1,0:T(8,128)(2,1)S(1)}, u32[]{:S(2)}) copy-start(bf16[1,1,3,3,144,1536]{5,4,3,2,1,0:T(8,128)(2,1)S(1)} %pad_maximum_fusion) | copy-start | bytes 11943940
  63.0 7.9 %copy-start.11 = (f32[1296,144]{0,1:T(8,128)}, f32[1296,144]{0,1:T(8,128)S(1)}, u32[]{:S(2)}) copy-start(f32[1296,144]{0,1:T(8,128)S(1)} %get-tuple-element.59) | copy-start | bytes 2239492
  63.4 8.6 %copy-start.13 = (f32[1296,144]{0,1:T(8,128)}, f32[1296,144]{0,1:T(8,128)S(1)}, u32[]{:S(2)}) copy-start(f32[1296,144]{0,1:T(8,128)S(1)} %get-tuple-element.57) | copy-start | bytes 2239492
  67.7 27.9 %copy-start.15 = (bf16[144,1296]{1,0:T(8,128)(2,1)}, bf16[144,1296]{1,0:T(8,128)(2,1)S(1)}, u32[]{:S(2)}) copy-start(bf16[144,1296]{1,0:T(8,128)(2,1)S(1)} %fusion.26) | copy-start | bytes 1119748
  79.7 15.5 %copy-start.17 = (bf16[144,1296]{1,0:T(8,128)(2,1)S(1)}, bf16[144,1296]{1,0:T(8,128)(2,1)}, u32[]{:S(2)}) copy-start(bf16[144,1296]{1,0:T(8,128)(2,1)} %fusion.25) | copy-start | bytes 1119748
  79.7 76.0 %all-to-all-start = ((bf16[8,192,768]{2,1,0:T(8,128)(2,1)}), bf16[8,192,768]{2,1,0:T(8,128)(2,1)}, u32[]{:S(2)}, u32[]{:S(2)}) async-start(bf16[8,192,768]{2,1,0:T(8,128)(2,1)} %bitcast.125), calls=%async_computation | async-start | bytes 4718592 | tf_op jit(solution)/shard_map/all_to_all | solution.py:39
  98.9 8.7 %copy-start.20 = (bf16[144,1296]{1,0:T(8,128)(2,1)S(1)}, bf16[144,1296]{1,0:T(8,128)(2,1)}, u32[]{:S(2)}) copy-start(bf16[144,1296]{1,0:T(8,128)(2,1)} %fusion.22) | copy-start | bytes 1119748
  99.4 9.5 %copy-start.19 = (bf16[144,1296]{1,0:T(8,128)(2,1)S(1)}, bf16[144,1296]{1,0:T(8,128)(2,1)}, u32[]{:S(2)}) copy-start(bf16[144,1296]{1,0:T(8,128)(2,1)} %fusion.23) | copy-start | bytes 1119748
  99.4 10.8 %copy-start.18 = (bf16[144,1296]{1,0:T(8,128)(2,1)S(1)}, bf16[144,1296]{1,0:T(8,128)(2,1)}, u32[]{:S(2)}) copy-start(bf16[144,1296]{1,0:T(8,128)(2,1)} %fusion.24) | copy-start | bytes 1119748
  99.8 46.7 %collective-permute-start.4 = (bf16[1,3,144,1536]{3,2,1,0:T(8,128)(2,1)S(1)}, bf16[1,3,144,1536]{3,2,1,0:T(8,128)(2,1)S(1)}, u32[]{:S(2)}, u32[]{:S(2)}) collective-permute-start(bf16[1,3,144,1536]{3,2,1,0:T(8,128)(2,1)S(1)} %get-tuple-element.12), channel_id=1, source_target_pairs={{1,0},{2,1},{3,2},{4,3},{5,4},{6,5},{7,6},{9,8},{10,9},{11,10},{12... | collective-permute-start | bytes 3981320 | tf_op jit(solution)/shard_map/ppermute | solution.py:15
  101.7 44.7 %collective-permute-start.5 = (bf16[1,3,144,1536]{3,2,1,0:T(8,128)(2,1)S(1)}, bf16[1,3,144,1536]{3,2,1,0:T(8,128)(2,1)S(1)}, u32[]{:S(2)}, u32[]{:S(2)}) collective-permute-start(bf16[1,3,144,1536]{3,2,1,0:T(8,128)(2,1)S(1)} %get-tuple-element.13), channel_id=1, source_target_pairs={{0,1},{1,2},{2,3},{3,4},{4,5},{5,6},{6,7},{8,9},{9,10},{10,11},{11... | collective-permute-start | bytes 3981320 | tf_op jit(solution)/shard_map/ppermute | solution.py:15
  111.5 35.0 %copy-start.25 = (bf16[144,768]{1,0:T(8,128)(2,1)}, bf16[144,768]{1,0:T(8,128)(2,1)S(1)}, u32[]{:S(2)}) copy-start(bf16[144,768]{1,0:T(8,128)(2,1)S(1)} %fusion.34) | copy-start | bytes 663556
  148.7 21.8 %copy-start.16 = (bf16[144,1296]{1,0:T(8,128)(2,1)S(1)}, bf16[144,1296]{1,0:T(8,128)(2,1)}, u32[]{:S(2)}) copy-start(bf16[144,1296]{1,0:T(8,128)(2,1)} %copy-done.15) | copy-start | bytes 1119748
  149.7 22.7 %collective-permute-start.6 = (bf16[1,144,1536]{2,1,0:T(8,128)(2,1)}, bf16[1,144,1536]{2,1,0:T(8,128)(2,1)}, u32[]{:S(2)}, u32[]{:S(2)}) collective-permute-start(bf16[1,144,1536]{2,1,0:T(8,128)(2,1)} %get-tuple-element.14), channel_id=1, source_target_pairs={{8,0},{16,8},{24,16},{9,1},{17,9},{25,17},{10,2},{18,10},{26,18},{... | collective-permute-start | bytes 1327112 | tf_op jit(solution)/shard_map/ppermute | solution.py:15
  150.9 21.4 %collective-permute-start.7 = (bf16[1,144,1536]{2,1,0:T(8,128)(2,1)}, bf16[1,144,1536]{2,1,0:T(8,128)(2,1)}, u32[]{:S(2)}, u32[]{:S(2)}) collective-permute-start(bf16[1,144,1536]{2,1,0:T(8,128)(2,1)} %get-tuple-element.15), channel_id=1, source_target_pairs={{0,8},{8,16},{16,24},{1,9},{9,17},{17,25},{2,10},{10,18},{18,26},{... | collective-permute-start | bytes 1327112 | tf_op jit(solution)/shard_map/ppermute | solution.py:15
  158.8 32.1 %all-to-all-start.1 = ((f32[32,6,768]{2,1,0:T(8,128)}), f32[32,6,768]{2,1,0:T(8,128)S(1)}, u32[]{:S(2)}, u32[]{:S(2)}) async-start(f32[32,6,768]{2,1,0:T(8,128)} %reshape.621), calls=%async_computation.1 | async-start | bytes 1572864 | tf_op jit(solution)/shard_map/all_to_all | solution.py:45
  (12 other events, 55.6 us)
where the time goes:
time: 193 us; the launch traced here: 191 us
  waiting for transfers between devices  62 us (32%)
  starting transfers between devices  45.7 us (24%)
  matrix products  31.4 us (16%)
  other arithmetic  20.7 us (11%)
  between operations  16.4 us (8%)
  local copies, waits for them, and re-layouts  15.2 us (8%)
    ppermute x4, waiting for transfers between devices, shifted(): return lax.ppermute(block, axis, route)  35 us
    all_to_all x1, waiting for transfers between devices, sum_at_owner(): parts = lax.all_to_all(split_up(array, dim, size), axis, 0, 0, tiled=True)  16.1 us
    ppermute x4, starting transfers between devices, shifted(): return lax.ppermute(block, axis, route)  12.7 us
    all_to_all x1, starting transfers between devices, sum_at_owner(): parts = lax.all_to_all(split_up(array, dim, size), axis, 0, 0, tiled=True)  9.75 us
    all_to_all x1, starting transfers between devices, sent_and_summed(): parts = lax.all_to_all(split_up(array, dim, size), axis, 0, 0, tiled=True)  9.69 us
    ppermute x2, waiting for transfers between devices, padded_2(): after = lax.ppermute(initial, axis, down)  9.57 us
    dot_general x6, matrix products, shards(): jnp.dot(grad_scores, key_head, preferred_element_type=jnp.float32)  8.88 us
    ppermute x2, starting transfers between devices, padded_2(): before = lax.ppermute(last, axis, up)  7.35 us
  transfers between devices with their start and end apart: 10, of which 4 were waited for; matrix products, arithmetic and copies ran while one was open for 21% of the time, Pallas kernels for 0%

commit v1 on v0

v1 whole, which is shorter than its diff:
```python
import math

import jax
import jax.numpy as jnp
from jax import lax
from jax.experimental import pallas as pl
from jax.experimental.pallas import tpu as pltpu
from jax.sharding import PartitionSpec as P

HEADS = 6
HD = 128
TILE = 144
SENT = HEADS - 1
ROWS = 3 * TILE
F32 = jnp.float32
BF16 = jnp.bfloat16
SCALE = 1.0 / math.sqrt(HD)
SCALE2 = SCALE * math.log2(math.e)
LOW = -1e30

SMEM = pl.BlockSpec(memory_space=pltpu.SMEM)
VMEM = pl.BlockSpec(memory_space=pltpu.VMEM)


def nt_dot(a, b):
    return lax.dot_general(a, b, (((1,), (1,)), ((), ())), preferred_element_type=F32)


def tn_dot(a, b):
    return lax.dot_general(a, b, (((0,), (0,)), ((), ())), preferred_element_type=F32)


def nn_dot(a, b):
    return jnp.dot(a, b, preferred_element_type=F32)


def lone_head(reaches):
    lone = jnp.int32(HEADS)
    for head in reversed(range(HEADS)):
        total = reaches[head, 0]
        for side in range(1, 6):
            total = total + reaches[head, side]
        lone = jnp.where(total == 0, jnp.int32(head), lone)
    return lone


def columns(head):
    return pl.ds(pl.multiple_of(head * HD, HD), HD)


def head_of(slot, lone):
    return slot + (slot >= lone).astype(jnp.int32)


def biases(reaches, place, head):
    row, col = place[0], place[1]
    row_count, col_count = place[2], place[3]
    up = jnp.where((reaches[head, 2] > 0) & (row > 0), 0.0, LOW)
    down = jnp.where((reaches[head, 3] > 0) & (row < row_count - 1), 0.0, LOW)
    left = jnp.where((reaches[head, 4] > 0) & (col > 0), 0.0, LOW)
    right = jnp.where((reaches[head, 5] > 0) & (col < col_count - 1), 0.0, LOW)
    lane = lax.broadcasted_iota(jnp.int32, (1, ROWS), 1)
    by_row = jnp.where(lane < TILE, up, jnp.where(lane < 2 * TILE, 0.0, down))
    return (jnp.minimum(by_row, left), by_row, jnp.minimum(by_row, right))


def pack_kernel(reaches, keys, values, packed):
    lone = lone_head(reaches)
    for slot in range(SENT):
        cols = columns(head_of(jnp.int32(slot), lone))
        packed[slot, :, :HD] = keys[:, cols]
        packed[slot, :, HD:] = values[:, cols]


def forward_kernel(reaches, place, queries, keys, values, left, mid, right, attended, norms):
    lone = lone_head(reaches)

    def one(slot, carry):
        head = head_of(slot, lone)
        cols = columns(head)
        query = queries[:, cols]
        scores = [
            nt_dot(query, block[slot, :, :HD]) + bias
            for block, bias in zip((left, mid, right), biases(reaches, place, head))
        ]
        peak = jnp.max(jnp.maximum(jnp.maximum(scores[0], scores[1]), scores[2]), axis=1, keepdims=True)
        terms = [jnp.exp2((s - peak) * SCALE2) for s in scores]
        total = jnp.sum(terms[0] + terms[1] + terms[2], axis=1, keepdims=True)
        sums = sum(
            nn_dot(t.astype(BF16), block[slot, :, HD:]) for t, block in zip(terms, (left, mid, right))
        )
        attended[:, cols] = (sums / total).astype(BF16)
        norms[slot] = jnp.broadcast_to(peak * SCALE2 + jnp.log2(total), (TILE, HD))
        return carry

    lax.fori_loop(0, SENT, one, 0)
    cols = columns(lone)
    scores = nt_dot(queries[:, cols], keys[:, cols])
    peak = jnp.max(scores, axis=1, keepdims=True)
    terms = jnp.exp2((scores - peak) * SCALE2)
    total = jnp.sum(terms, axis=1, keepdims=True)
    attended[:, cols] = (nn_dot(terms.astype(BF16), values[:, cols]) / total).astype(BF16)
    norms[SENT] = jnp.broadcast_to(peak * SCALE2 + jnp.log2(total), (TILE, HD))


def backward_kernel(
    reaches, place, queries, keys, values, grads, attended, norms, left, mid, right,
    grad_query, g_left, g_mid, g_right, g_lone,
):
    lone = lone_head(reaches)

    def one(slot, carry):
        head = head_of(slot, lone)
        cols = columns(head)
        query = queries[:, cols]
        grad = grads[:, cols]
        norm = norms[slot][:, :1]
        delta = jnp.sum(grad.astype(F32) * attended[:, cols].astype(F32), axis=1, keepdims=True)
        total = jnp.zeros((TILE, HD), F32)
        for block, bias, out in zip(
            (left, mid, right), biases(reaches, place, head), (g_left, g_mid, g_right)
        ):
            key = block[slot, :, :HD]
            value = block[slot, :, HD:]
            probs = jnp.exp2((nt_dot(query, key) + bias) * SCALE2 - norm)
            slopes = (probs * (nt_dot(grad, value) - delta)).astype(BF16)
            total = total + nn_dot(slopes, key)
            out[slot, :, :HD] = (tn_dot(slopes, query) * SCALE).astype(BF16)
            out[slot, :, HD:] = tn_dot(probs.astype(BF16), grad).astype(BF16)
        grad_query[:, cols] = (total * SCALE).astype(BF16)
        return carry

    lax.fori_loop(0, SENT, one, 0)
    cols = columns(lone)
    query = queries[:, cols]
    grad = grads[:, cols]
    key = keys[:, cols]
    delta = jnp.sum(grad.astype(F32) * attended[:, cols].astype(F32), axis=1, keepdims=True)
    probs = jnp.exp2(nt_dot(query, key) * SCALE2 - norms[SENT][:, :1])
    slopes = (probs * (nt_dot(grad, values[:, cols]) - delta)).astype(BF16)
    grad_query[:, cols] = (nn_dot(slopes, key) * SCALE).astype(BF16)
    g_lone[:, :HD] = (tn_dot(slopes, query) * SCALE).astype(BF16)
    g_lone[:, HD:] = tn_dot(probs.astype(BF16), grad).astype(BF16)


def width_sum_kernel(g_mid, from_right, from_left, own, to_up, to_down):
    for slot in range(SENT):
        total = (
            g_mid[slot].astype(F32) + from_right[slot].astype(F32) + from_left[slot].astype(F32)
        )
        to_up[slot] = total[:TILE].astype(BF16)
        own[slot] = total[TILE : 2 * TILE]
        to_down[slot] = total[2 * TILE :].astype(BF16)


def height_sum_kernel(reaches, own, from_down, from_up, g_lone, grad_key, grad_value):
    lone = lone_head(reaches)
    for slot in range(SENT):
        cols = columns(head_of(jnp.int32(slot), lone))
        total = own[slot] + from_down[slot].astype(F32) + from_up[slot].astype(F32)
        grad_key[:, cols] = total[:, :HD].astype(BF16)
        grad_value[:, cols] = total[:, HD:].astype(BF16)
    cols = columns(lone)
    grad_key[:, cols] = g_lone[:, :HD]
    grad_value[:, cols] = g_lone[:, HD:]


def call(kernel, outs, specs, flops=0):
    return pl.pallas_call(
        kernel,
        out_shape=[jax.ShapeDtypeStruct(shape, dtype) for shape, dtype in outs],
        in_specs=specs,
        out_specs=[VMEM] * len(outs),
        cost_estimate=pl.CostEstimate(flops=flops, transcendentals=0, bytes_accessed=1 << 20),
    )


def shifted(block, axis, distance):
    devices = range(lax.axis_size(axis))
    route = [(i - distance, i) for i in devices if i - distance in devices]
    return lax.ppermute(block, axis, route)


def row_order(model_width, dp, ha, wa):
    import numpy as np

    width = model_width // (dp * ha * wa)
    index = np.arange(model_width).reshape(2, dp // 2, ha, wa // 2, 2, width)
    return index.transpose(4, 1, 2, 0, 3, 5).reshape(-1)


def exchanged(array, axes, groups, size):
    parts = array.reshape(size, array.shape[0] // size, array.shape[1])
    parts = lax.all_to_all(parts, axes, 0, 0, axis_index_groups=groups, tiled=True)
    return jnp.sum(parts.astype(F32), axis=0)


def shards(queries, key_tiles, value_tiles, out_grad, w_out, reaches):
    shape = queries.shape
    width = shape[5]
    model_width = out_grad.shape[5]
    dp, ha, wa = (lax.axis_size(axis) for axis in ("dp", "ha", "wa"))
    place = jnp.stack(
        [lax.axis_index("ha"), lax.axis_index("wa"), jnp.int32(ha), jnp.int32(wa)]
    ).astype(jnp.int32)
    queries = queries.reshape(TILE, width)
    keys = key_tiles.reshape(TILE, width)
    values = value_tiles.reshape(TILE, width)
    grad_rows = out_grad.reshape(TILE, model_width)

    tile = (SENT, TILE, 2 * HD)
    rows = (SENT, ROWS, 2 * HD)
    (packed,) = call(pack_kernel, [(tile, BF16)], [SMEM, VMEM, VMEM])(reaches, keys, values)
    up = shifted(packed, "ha", 1)
    down = shifted(packed, "ha", -1)
    mid = jnp.concatenate([up, packed, down], axis=1)
    left = shifted(mid, "wa", 1)
    right = shifted(mid, "wa", -1)

    grads = jnp.dot(grad_rows, w_out, preferred_element_type=F32).astype(BF16)
    order = row_order(model_width, dp, ha, wa)
    select = (jnp.arange(model_width)[:, None] == order[None, :]).astype(BF16)
    sorted_rows = jnp.dot(grad_rows, select, preferred_element_type=F32).astype(BF16)
    halves = sorted_rows.reshape(TILE, 2, model_width // 2)
    core = lax.axis_index("wa") % 2
    pair = [(i, i ^ 1) for i in range(wa)]
    mine = jnp.where(core == 0, halves[:, 0], halves[:, 1])
    other = jnp.where(core == 0, halves[:, 1], halves[:, 0])
    partner_rows = lax.ppermute(other, "wa", pair)
    both_rows = jnp.concatenate([mine, partner_rows], axis=0)

    attended, norms = call(
        forward_kernel,
        [((TILE, width), BF16), ((HEADS, TILE, HD), F32)],
        [SMEM, SMEM] + [VMEM] * 6,
        flops=10**9,
    )(reaches, place, queries, keys, values, left, mid, right)

    both_attended = jnp.concatenate([attended, lax.ppermute(attended, "wa", pair)], axis=0)
    product = lax.dot_general(
        both_rows, both_attended, (((0,), (0,)), ((), ())), preferred_element_type=F32
    ).astype(BF16)
    half = dp // 2
    x_groups = [[z * half + x for x in range(half)] for z in range(2)]
    summed = exchanged(product, "dp", x_groups, half).astype(BF16)
    summed = exchanged(summed, "ha", None, ha).astype(BF16)
    z_groups = [
        [(z * half + x) * wa + w * 2 + c for z in range(2) for w in range(wa // 2)]
        for x in range(half)
        for c in range(2)
    ]
    grad_w_out = exchanged(summed, ("dp", "wa"), z_groups, wa)

    grad_query, g_left, g_mid, g_right, g_lone = call(
        backward_kernel,
        [((TILE, width), BF16), (rows, BF16), (rows, BF16), (rows, BF16), ((TILE, 2 * HD), BF16)],
        [SMEM, SMEM] + [VMEM] * 9,
        flops=2 * 10**9,
    )(reaches, place, queries, keys, values, grads, attended, norms, left, mid, right)
    from_right = shifted(g_left, "wa", -1)
    from_left = shifted(g_right, "wa", 1)
    own, to_up, to_down = call(
        width_sum_kernel, [(tile, F32), (tile, BF16), (tile, BF16)], [VMEM] * 3
    )(g_mid, from_right, from_left)
    from_down = shifted(to_up, "ha", -1)
    from_up = shifted(to_down, "ha", 1)
    grad_key, grad_value = call(
        height_sum_kernel, [((TILE, width), BF16)] * 2, [SMEM] + [VMEM] * 4
    )(reaches, own, from_down, from_up, g_lone)
    return (
        grad_query.reshape(shape), grad_key.reshape(shape), grad_value.reshape(shape), grad_w_out,
    )


def solution(mesh):
    tiles = P("dp", None, "ha", "wa", None, None)
    return jax.shard_map(
        shards,
        mesh=mesh,
        in_specs=(tiles, tiles, tiles, tiles, P(), P()),
        out_specs=(tiles, tiles, tiles, P(("dp", "ha", "wa"), None)),
        check_vma=False,
    )
```

time: 193 us -> 122 us (0.63)
  the two profiles are of different devices: /device:TPU:1 before, /device:TPU:8 now
where the time goes in v1:
time: 122 us; the launch traced here: 121 us
  blocking collectives  37.1 us (30%)
  starting transfers between devices  34.4 us (28%)
  Pallas kernels  24.8 us (20%)
  waiting for transfers between devices  8.38 us (7%)
  matrix products  6.56 us (5%)
  local copies, waits for them, and re-layouts  4.75 us (4%)
  other arithmetic  4.12 us (3%)
    all_to_all x2, blocking collectives, exchanged(): lax.all_to_all(parts, axes, 0, 0, axis_index_groups=groups, tiled=True)  37.1 us
    ppermute x8, starting transfers between devices, shifted(): return lax.ppermute(block, axis, route)  20.8 us
    pallas_call x1, Pallas kernels, shards(): call(backward_kernel, [((TILE, width), BF16), (rows, BF16), (rows, BF16),...  10.3 us
    ppermute x8, waiting for transfers between devices, shifted(): return lax.ppermute(block, axis, route)  8.37 us
    pallas_call x1, Pallas kernels, shards(): call(forward_kernel, [((TILE, width), BF16), ((HEADS, TILE, HD), F32)], [...  7 us
    ppermute x1, starting transfers between devices, shards(): lax.ppermute(attended, 'wa', pair)  6.04 us
    all_to_all x1, starting transfers between devices, exchanged(): lax.all_to_all(parts, axes, 0, 0, axis_index_groups=groups, tiled=True)  5.03 us
    dot_general x1, matrix products, shards(): jnp.dot(grad_rows, select, preferred_element_type=F32).astype(BF16)  3.62 us
  transfers between devices with their start and end apart: 11, of which 2 were waited for; matrix products, arithmetic and copies ran while one was open for 11% of the time, Pallas kernels for 17%

profile of v1, /device:TPU:8, one launch (start us, length us, event | category | flops | bytes accessed | tf_op | source)
XLA Modules:
  0.0 120.9 jit_solution(1456508376738078960)
XLA Ops:
  0.6 2.0 %shard_map.102 = bf16[5,144,256]{2,1,0:T(8,128)(2,1)} custom-call(s32[6,6]{1,0:T(8,128)} %reaches.7, bf16[144,768]{1,0:T(8,128)(2,1)} %bitcast.24, bf16[144,768]{1,0:T(8,128)(2,1)} %bitcast.27), custom_call_target="tpu_custom_call" | custom-call | bytes 1048576 | tf_op jit(solution)/shard_map/pallas_call | solution.py:213
  2.7 4.2 %collective-permute-start.1 = (bf16[5,144,256]{2,1,0:T(8,128)(2,1)}, bf16[5,144,256]{2,1,0:T(8,128)(2,1)S(1)}, u32[]{:S(2)}, u32[]{:S(2)}) collective-permute-start(bf16[5,144,256]{2,1,0:T(8,128)(2,1)} %shard_map.102), channel_id=1, source_target_pairs={{8,0},{16,8},{24,16},{9,1},{17,9},{25,17},{10,2},{18,10},{26,18},{... | collective-permute-start | bytes 1105928 | tf_op jit(solution)/shard_map/ppermute | solution.py:181
  6.9 1.9 %collective-permute-start = (bf16[5,144,256]{2,1,0:T(8,128)(2,1)}, bf16[5,144,256]{2,1,0:T(8,128)(2,1)S(1)}, u32[]{:S(2)}, u32[]{:S(2)}) collective-permute-start(bf16[5,144,256]{2,1,0:T(8,128)(2,1)} %shard_map.102), channel_id=1, source_target_pairs={{0,8},{8,16},{16,24},{1,9},{9,17},{17,25},{2,10},{10,18},{18,26},{... | collective-permute-start | bytes 1105928 | tf_op jit(solution)/shard_map/ppermute | solution.py:181
  8.8 6.4 %collective-permute-done.1 = bf16[5,144,256]{2,1,0:T(8,128)(2,1)S(1)} collective-permute-done((bf16[5,144,256]{2,1,0:T(8,128)(2,1)}, bf16[5,144,256]{2,1,0:T(8,128)(2,1)S(1)}, u32[]{:S(2)}, u32[]{:S(2)}) %collective-permute-start.1) | collective-permute-done | bytes 368672 | tf_op jit(solution)/shard_map/ppermute | solution.py:181
  15.2 1.9 %collective-permute-done = bf16[5,144,256]{2,1,0:T(8,128)(2,1)S(1)} collective-permute-done((bf16[5,144,256]{2,1,0:T(8,128)(2,1)}, bf16[5,144,256]{2,1,0:T(8,128)(2,1)S(1)}, u32[]{:S(2)}, u32[]{:S(2)}) %collective-permute-start) | collective-permute-done | bytes 368672 | tf_op jit(solution)/shard_map/ppermute | solution.py:181
  18.2 2.3 %collective-permute-start.2 = (bf16[5,432,256]{2,1,0:T(8,128)(2,1)S(1)}, bf16[5,432,256]{2,1,0:T(8,128)(2,1)}, u32[]{:S(2)}, u32[]{:S(2)}) collective-permute-start(bf16[5,432,256]{2,1,0:T(8,128)(2,1)S(1)} %pad_maximum_fusion.mid), channel_id=1, source_target_pairs={{0,1},{1,2},{2,3},{3,4},{4,5},{5,6},{6,7},{8,9},{9,10},{10,11},{11... | collective-permute-start | bytes 3317768 | tf_op jit(solution)/shard_map/ppermute | solution.py:181
  20.5 1.3 %collective-permute-start.3 = (bf16[5,432,256]{2,1,0:T(8,128)(2,1)S(1)}, bf16[5,432,256]{2,1,0:T(8,128)(2,1)}, u32[]{:S(2)}, u32[]{:S(2)}) collective-permute-start(bf16[5,432,256]{2,1,0:T(8,128)(2,1)S(1)} %pad_maximum_fusion.mid), channel_id=1, source_target_pairs={{1,0},{2,1},{3,2},{4,3},{5,4},{6,5},{7,6},{9,8},{10,9},{11,10},{12... | collective-permute-start | bytes 3317768 | tf_op jit(solution)/shard_map/ppermute | solution.py:181
  21.9 3.6 %fusion.3 = bf16[144,1536]{1,0:T(8,128)(2,1)} fusion(s32[1536]{0:T(1024)S(1)} %copy-done.7, bf16[1,1,1,1,144,1536]{5,4,3,2,1,0:T(8,128)(2,1)} %param.10), kind=kOutput, calls=%fused_computation.4 | convolution fusion | flops 682057728 | bytes 890880 | tf_op jit(solution)/shard_map/dot_general | solution.py:223
  25.5 1.9 %reshape.52 = bf16[144,2,768]{2,1,0:T(2,128)(2,1)} reshape(bf16[144,1536]{1,0:T(8,128)(2,1)} %fusion.3) | data formatting | bytes 884736 | tf_op jit(solution)/shard_map/reshape | solution.py:224
  27.3 1.9 %fusion.13 = (bf16[144,1,768]{2,1,0:T(2,128)(2,1)S(1)}, bf16[144,1,768]{2,1,0:T(2,128)(2,1)S(1)}) fusion(bf16[144,2,768]{2,1,0:T(2,128)(2,1)} %reshape.52), kind=kLoop, calls=%fused_computation.21 | loop fusion | bytes 884736 | tf_op jit(solution)/shard_map/slice | solution.py:227
  30.1 2.4 %collective-permute-start.8 = (bf16[144,768]{1,0:T(8,128)(2,1)}, bf16[144,768]{1,0:T(8,128)(2,1)}, u32[]{:S(2)}, u32[]{:S(2)}) collective-permute-start(bf16[144,768]{1,0:T(8,128)(2,1)} %get-tuple-element.29), channel_id=1, source_target_pairs={{0,1},{1,0},{2,3},{3,2},{4,5},{5,4},{6,7},{7,6},{8,9},{9,8},{10,11... | collective-permute-start | bytes 663560 | tf_op jit(solution)/shard_map/ppermute | solution.py:229
  33.2 7.0 %shard_map.103 = (bf16[144,768]{1,0:T(8,128)(2,1)}, f32[6,144,128]{2,1,0:T(8,128)}) custom-call(s32[6,6]{1,0:T(8,128)} %reaches.7, s32[4]{0:T(128)} %pad_add_fusion.place, bf16[144,768]{1,0:T(8,128)(2,1)} %bitcast.30, bf16[144,768]{1,0:T(8,128)(2,1)} %bitcast.25, bf16[144,768]{1,0:T(8,128)(2,1)} %bitcast.28, ...), custom_call_target="tpu_custom_call" | custom-call | flops 1000000000 | bytes 1048576 | tf_op jit(solution)/shard_map/pallas_call | solution.py:232
  40.2 6.0 %collective-permute-start.9 = (bf16[144,768]{1,0:T(8,128)(2,1)}, bf16[144,768]{1,0:T(8,128)(2,1)S(1)}, u32[]{:S(2)}, u32[]{:S(2)}) collective-permute-start(bf16[144,768]{1,0:T(8,128)(2,1)} %get-tuple-element.16.attended), channel_id=1, source_target_pairs={{0,1},{1,0},{2,3},{3,2},{4,5},{5,4},{6,7},{7,6},{8,9},{9,8},{10,11... | collective-permute-start | bytes 663560 | tf_op jit(solution)/shard_map/ppermute | solution.py:239
  47.4 10.3 %shard_map.104 = (bf16[144,768]{1,0:T(8,128)(2,1)}, bf16[5,432,256]{2,1,0:T(8,128)(2,1)}, bf16[5,432,256]{2,1,0:T(8,128)(2,1)}, bf16[5,432,256]{2,1,0:T(8,128)(2,1)}, bf16[144,256]{1,0:T(8,128)(2,1)}) custom-call(s32[6,6]{1,0:T(8,128)} %reaches.7, s32[4]{0:T(128)} %pad_add_fusion.place, bf16[144,768]{1,0:T(8,128)(2,1)} %bitcast.31, ...), custom_call_target="tpu_custom_call" | custom-call | flops 2000000000 | bytes 1048576 | tf_op jit(solution)/shard_map/pallas_call | solution.py:254
  57.7 1.3 %collective-permute-start.4 = (bf16[5,432,256]{2,1,0:T(8,128)(2,1)}, bf16[5,432,256]{2,1,0:T(8,128)(2,1)}, u32[]{:S(2)}, u32[]{:S(2)}) collective-permute-start(bf16[5,432,256]{2,1,0:T(8,128)(2,1)} %get-tuple-element.20), channel_id=1, source_target_pairs={{1,0},{2,1},{3,2},{4,3},{5,4},{6,5},{7,6},{9,8},{10,9},{11,10},{12... | collective-permute-start | bytes 3317768 | tf_op jit(solution)/shard_map/ppermute | solution.py:181
  59.0 4.0 %collective-permute-start.5 = (bf16[5,432,256]{2,1,0:T(8,128)(2,1)}, bf16[5,432,256]{2,1,0:T(8,128)(2,1)}, u32[]{:S(2)}, u32[]{:S(2)}) collective-permute-start(bf16[5,432,256]{2,1,0:T(8,128)(2,1)} %get-tuple-element.21), channel_id=1, source_target_pairs={{0,1},{1,2},{2,3},{3,4},{4,5},{5,6},{6,7},{8,9},{9,10},{10,11},{11... | collective-permute-start | bytes 3317768 | tf_op jit(solution)/shard_map/ppermute | solution.py:181
  63.0 1.7 %convolution_convert_fusion = bf16[768,768]{1,0:T(8,128)(2,1)S(1)} fusion(bf16[144,768]{1,0:T(8,128)(2,1)} %collective-permute-done.8, bf16[144,768]{1,0:T(8,128)(2,1)S(1)} %copy-done.5, bf16[144,768]{1,0:T(8,128)(2,1)S(1)} %collective-permute-done.9, bf16[144,768]{1,0:T(8,128)(2,1)S(1)} %copy-done.6), kind=kOutput, calls=%fused_computation.5 | convolution fusion | flops 342097920 | bytes 2064384 | tf_op jit(solution)/shard_map/dot_general | solution.py:240
  64.8 21.3 %all_to_all.15 = bf16[4,192,768]{2,1,0:T(8,128)(2,1)S(1)} all-to-all(bf16[4,192,768]{2,1,0:T(8,128)(2,1)S(1)} %bitcast.22), channel_id=1, replica_groups={{0,32,64,96},{128,160,192,224},{1,33,65,97},{129,161,193,225},{2,34,66,..., dimensions={0} | all-to-all | bytes 2359296 | tf_op jit(solution)/shard_map/all_to_all | solution.py:194
  87.0 5.0 %all-to-all-start.1 = ((bf16[4,48,768]{2,1,0:T(8,128)(2,1)}), bf16[4,48,768]{2,1,0:T(8,128)(2,1)S(1)}, u32[]{:S(2)}, u32[]{:S(2)}) async-start(bf16[4,48,768]{2,1,0:T(8,128)(2,1)} %bitcast.23), calls=%async_computation.1 | async-start | bytes 589824 | tf_op jit(solution)/shard_map/all_to_all | solution.py:194
  92.1 3.3 %shard_map.105 = (f32[5,144,256]{2,1,0:T(8,128)}, bf16[5,144,256]{2,1,0:T(8,128)(2,1)}, bf16[5,144,256]{2,1,0:T(8,128)(2,1)}) custom-call(bf16[5,432,256]{2,1,0:T(8,128)(2,1)} %get-tuple-element.19.g_mid, bf16[5,432,256]{2,1,0:T(8,128)(2,1)} %collective-permute-done.4.from_right, bf16[5,432,256]{2,1,0:T(8,128)(2,1)} %collective-permute-done.5.from_left), custom_call_target="tpu_custom_call" | custom-call | bytes 1048576 | tf_op jit(solution)/shard_map/pallas_call | solution.py:262
  95.3 1.9 %collective-permute-start.6 = (bf16[5,144,256]{2,1,0:T(8,128)(2,1)}, bf16[5,144,256]{2,1,0:T(8,128)(2,1)S(1)}, u32[]{:S(2)}, u32[]{:S(2)}) collective-permute-start(bf16[5,144,256]{2,1,0:T(8,128)(2,1)} %get-tuple-element.23), channel_id=1, source_target_pairs={{8,0},{16,8},{24,16},{9,1},{17,9},{25,17},{10,2},{18,10},{26,18},{... | collective-permute-start | bytes 1105928 | tf_op jit(solution)/shard_map/ppermute | solution.py:181
  97.3 3.9 %collective-permute-start.7 = (bf16[5,144,256]{2,1,0:T(8,128)(2,1)}, bf16[5,144,256]{2,1,0:T(8,128)(2,1)S(1)}, u32[]{:S(2)}, u32[]{:S(2)}) collective-permute-start(bf16[5,144,256]{2,1,0:T(8,128)(2,1)} %get-tuple-element.24), channel_id=1, source_target_pairs={{0,8},{8,16},{16,24},{1,9},{9,17},{17,25},{2,10},{10,18},{18,26},{... | collective-permute-start | bytes 1105928 | tf_op jit(solution)/shard_map/ppermute | solution.py:181
  101.3 15.8 %all_to_all.16 = bf16[8,6,768]{2,1,0:T(8,128)(2,1)S(1)} all-to-all(bf16[8,6,768]{2,1,0:T(8,128)(2,1)S(1)} %reshape.55), channel_id=1, replica_groups={{0,2,4,6,128,130,132,134},{1,3,5,7,129,131,133,135},{32,34,36,38,160,16..., dimensions={0} | all-to-all | bytes 147456 | tf_op jit(solution)/shard_map/all_to_all | solution.py:194
  118.7 2.2 %shard_map.106 = (bf16[144,768]{1,0:T(8,128)(2,1)}, bf16[144,768]{1,0:T(8,128)(2,1)}) custom-call(s32[6,6]{1,0:T(8,128)} %reaches.7, f32[5,144,256]{2,1,0:T(8,128)} %get-tuple-element.22.own, bf16[5,144,256]{2,1,0:T(8,128)(2,1)} %copy-done.3, bf16[5,144,256]{2,1,0:T(8,128)(2,1)} %copy-done.4, bf16[144,256]{1,0:T(8,128)(2,1)} %get-tuple-element.25.g_lone), custom_call_target="tpu_custom_call" | custom-call | bytes 1048576 | tf_op jit(solution)/shard_map/pallas_call | solution.py:267
  (33 shorter events, 6.3 us)
Async XLA Ops:
  0.6 45.6 %copy-start = (bf16[1536,768]{1,0:T(8,128)(2,1)S(1)}, bf16[1536,768]{1,0:T(8,128)(2,1)}, u32[]{:S(2)}) copy-start(bf16[1536,768]{1,0:T(8,128)(2,1)} %param.11) | copy-start | bytes 7077892
  2.7 19.2 %copy-start.7 = (s32[1536]{0:T(1024)S(1)}, s32[1536]{0:T(1024)}, u32[]{:S(2)}) copy-start(s32[1536]{0:T(1024)} %constant.38) | copy-start | bytes 18436
  2.7 12.6 %collective-permute-start.1 = (bf16[5,144,256]{2,1,0:T(8,128)(2,1)}, bf16[5,144,256]{2,1,0:T(8,128)(2,1)S(1)}, u32[]{:S(2)}, u32[]{:S(2)}) collective-permute-start(bf16[5,144,256]{2,1,0:T(8,128)(2,1)} %shard_map.102), channel_id=1, source_target_pairs={{8,0},{16,8},{24,16},{9,1},{17,9},{25,17},{10,2},{18,10},{26,18},{... | collective-permute-start | bytes 1105928 | tf_op jit(solution)/shard_map/ppermute | solution.py:181
  6.9 10.3 %collective-permute-start = (bf16[5,144,256]{2,1,0:T(8,128)(2,1)}, bf16[5,144,256]{2,1,0:T(8,128)(2,1)S(1)}, u32[]{:S(2)}, u32[]{:S(2)}) collective-permute-start(bf16[5,144,256]{2,1,0:T(8,128)(2,1)} %shard_map.102), channel_id=1, source_target_pairs={{0,8},{8,16},{16,24},{1,9},{9,17},{17,25},{2,10},{10,18},{18,26},{... | collective-permute-start | bytes 1105928 | tf_op jit(solution)/shard_map/ppermute | solution.py:181
  18.2 7.2 %copy-start.1 = (bf16[5,432,256]{2,1,0:T(8,128)(2,1)}, bf16[5,432,256]{2,1,0:T(8,128)(2,1)S(1)}, u32[]{:S(2)}) copy-start(bf16[5,432,256]{2,1,0:T(8,128)(2,1)S(1)} %pad_maximum_fusion.mid) | copy-start | bytes 3317764
  18.2 14.9 %collective-permute-start.2 = (bf16[5,432,256]{2,1,0:T(8,128)(2,1)S(1)}, bf16[5,432,256]{2,1,0:T(8,128)(2,1)}, u32[]{:S(2)}, u32[]{:S(2)}) collective-permute-start(bf16[5,432,256]{2,1,0:T(8,128)(2,1)S(1)} %pad_maximum_fusion.mid), channel_id=1, source_target_pairs={{0,1},{1,2},{2,3},{3,4},{4,5},{5,6},{6,7},{8,9},{9,10},{10,11},{11... | collective-permute-start | bytes 3317768 | tf_op jit(solution)/shard_map/ppermute | solution.py:181
  20.5 12.6 %collective-permute-start.3 = (bf16[5,432,256]{2,1,0:T(8,128)(2,1)S(1)}, bf16[5,432,256]{2,1,0:T(8,128)(2,1)}, u32[]{:S(2)}, u32[]{:S(2)}) collective-permute-start(bf16[5,432,256]{2,1,0:T(8,128)(2,1)S(1)} %pad_maximum_fusion.mid), channel_id=1, source_target_pairs={{1,0},{2,1},{3,2},{4,3},{5,4},{6,5},{7,6},{9,8},{10,9},{11,10},{12... | collective-permute-start | bytes 3317768 | tf_op jit(solution)/shard_map/ppermute | solution.py:181
  30.1 32.9 %collective-permute-start.8 = (bf16[144,768]{1,0:T(8,128)(2,1)}, bf16[144,768]{1,0:T(8,128)(2,1)}, u32[]{:S(2)}, u32[]{:S(2)}) collective-permute-start(bf16[144,768]{1,0:T(8,128)(2,1)} %get-tuple-element.29), channel_id=1, source_target_pairs={{0,1},{1,0},{2,3},{3,2},{4,5},{5,4},{6,7},{7,6},{8,9},{9,8},{10,11... | collective-permute-start | bytes 663560 | tf_op jit(solution)/shard_map/ppermute | solution.py:229
  33.2 13.0 %copy-start.2 = (bf16[1,1,1,1,144,1536]{5,4,3,2,1,0:T(8,128)(2,1)S(1)}, bf16[1,1,1,1,144,1536]{5,4,3,2,1,0:T(8,128)(2,1)}, u32[]{:S(2)}) copy-start(bf16[1,1,1,1,144,1536]{5,4,3,2,1,0:T(8,128)(2,1)} %param.10) | copy-start | bytes 1327108
  40.2 22.9 %collective-permute-start.9 = (bf16[144,768]{1,0:T(8,128)(2,1)}, bf16[144,768]{1,0:T(8,128)(2,1)S(1)}, u32[]{:S(2)}, u32[]{:S(2)}) collective-permute-start(bf16[144,768]{1,0:T(8,128)(2,1)} %get-tuple-element.16.attended), channel_id=1, source_target_pairs={{0,1},{1,0},{2,3},{3,2},{4,5},{5,4},{6,7},{7,6},{8,9},{9,8},{10,11... | collective-permute-start | bytes 663560 | tf_op jit(solution)/shard_map/ppermute | solution.py:239
  47.4 15.6 %copy-start.5 = (bf16[144,768]{1,0:T(8,128)(2,1)S(1)}, bf16[144,768]{1,0:T(8,128)(2,1)}, u32[]{:S(2)}) copy-start(bf16[144,768]{1,0:T(8,128)(2,1)} %get-tuple-element.28) | copy-start | bytes 663556
  47.4 15.6 %copy-start.6 = (bf16[144,768]{1,0:T(8,128)(2,1)S(1)}, bf16[144,768]{1,0:T(8,128)(2,1)}, u32[]{:S(2)}) copy-start(bf16[144,768]{1,0:T(8,128)(2,1)} %get-tuple-element.16.attended) | copy-start | bytes 663556
  57.7 34.4 %collective-permute-start.4 = (bf16[5,432,256]{2,1,0:T(8,128)(2,1)}, bf16[5,432,256]{2,1,0:T(8,128)(2,1)}, u32[]{:S(2)}, u32[]{:S(2)}) collective-permute-start(bf16[5,432,256]{2,1,0:T(8,128)(2,1)} %get-tuple-element.20), channel_id=1, source_target_pairs={{1,0},{2,1},{3,2},{4,3},{5,4},{6,5},{7,6},{9,8},{10,9},{11,10},{12... | collective-permute-start | bytes 3317768 | tf_op jit(solution)/shard_map/ppermute | solution.py:181
  59.0 33.1 %collective-permute-start.5 = (bf16[5,432,256]{2,1,0:T(8,128)(2,1)}, bf16[5,432,256]{2,1,0:T(8,128)(2,1)}, u32[]{:S(2)}, u32[]{:S(2)}) collective-permute-start(bf16[5,432,256]{2,1,0:T(8,128)(2,1)} %get-tuple-element.21), channel_id=1, source_target_pairs={{0,1},{1,2},{2,3},{3,4},{4,5},{5,6},{6,7},{8,9},{9,10},{10,11},{11... | collective-permute-start | bytes 3317768 | tf_op jit(solution)/shard_map/ppermute | solution.py:181
  87.0 14.1 %all-to-all-start.1 = ((bf16[4,48,768]{2,1,0:T(8,128)(2,1)}), bf16[4,48,768]{2,1,0:T(8,128)(2,1)S(1)}, u32[]{:S(2)}, u32[]{:S(2)}) async-start(bf16[4,48,768]{2,1,0:T(8,128)(2,1)} %bitcast.23), calls=%async_computation.1 | async-start | bytes 589824 | tf_op jit(solution)/shard_map/all_to_all | solution.py:194
  95.3 22.4 %collective-permute-start.6 = (bf16[5,144,256]{2,1,0:T(8,128)(2,1)}, bf16[5,144,256]{2,1,0:T(8,128)(2,1)S(1)}, u32[]{:S(2)}, u32[]{:S(2)}) collective-permute-start(bf16[5,144,256]{2,1,0:T(8,128)(2,1)} %get-tuple-element.23), channel_id=1, source_target_pairs={{8,0},{16,8},{24,16},{9,1},{17,9},{25,17},{10,2},{18,10},{26,18},{... | collective-permute-start | bytes 1105928 | tf_op jit(solution)/shard_map/ppermute | solution.py:181
  97.3 20.5 %collective-permute-start.7 = (bf16[5,144,256]{2,1,0:T(8,128)(2,1)}, bf16[5,144,256]{2,1,0:T(8,128)(2,1)S(1)}, u32[]{:S(2)}, u32[]{:S(2)}) collective-permute-start(bf16[5,144,256]{2,1,0:T(8,128)(2,1)} %get-tuple-element.24), channel_id=1, source_target_pairs={{0,8},{8,16},{16,24},{1,9},{9,17},{17,25},{2,10},{10,18},{18,26},{... | collective-permute-start | bytes 1105928 | tf_op jit(solution)/shard_map/ppermute | solution.py:181
  117.8 0.7 copy-start.3
  117.8 0.9 copy-start.4
